TPU v7x, 32 devices: a whole 2x2x4 slice. The times are simulated.
32 devices in a mesh: dp: 8 (over z, x), tensor: 4 (over y, core).
Axes of the slice: x: 2, y: 2, z: 4, core: 2. Of those that a mesh axis runs over, the one named last changes fastest.
Arguments:
- patches: bfloat16 [16384, 768], P(('dp', 'tensor')), may hold values from -6 to 6
- counts: int32 [8, 3], P('dp'), may hold values from 1 to 2, as said below
- norm_gain: float32 [2, 768], replicated, may hold values from 0.5 to 1.5
- norm_bias: float32 [2, 768], replicated, may hold values from -3 to 3
- w_qkv: bfloat16 [768, 3, 768], P(None, None, 'tensor'), may hold values from -0.21875 to 0.21875
- b_qv: float32 [2, 768], P(None, 'tensor'), may hold values from -3 to 3
- w_out: bfloat16 [768, 768], P('tensor'), may hold values from -0.625 to 0.625
- out_bias: float32 [2, 768], replicated, may hold values from -3 to 3
- w_up: bfloat16 [768, 3072], P(None, 'tensor'), may hold values from -0.21875 to 0.21875
- b_up: float32 [3072], P('tensor'), may hold values from -3 to 3
- w_down: bfloat16 [3072, 768], P('tensor'), may hold values from -0.109375 to 0.109375
- cotangent: bfloat16 [16384, 768], P(('dp', 'tensor')), may hold values from -6 to 6
Outputs:
- encoded: bfloat16 [16384, 768], P(('dp', 'tensor'))
- patches_grad: bfloat16 [16384, 768], P(('dp', 'tensor'))
- norm_gain_grad: float32 [2, 768], replicated
- norm_bias_grad: float32 [2, 768], replicated
- w_qkv_grad: float32 [768, 3, 768], P('dp', None, 'tensor')
- b_qv_grad: float32 [2, 768], replicated
- w_out_grad: float32 [768, 768], P('tensor', 'dp')
- out_bias_grad: float32 [2, 768], replicated
- w_up_grad: float32 [768, 3072], P('dp', 'tensor')
- b_up_grad: float32 [3072], replicated
- w_down_grad: float32 [3072, 768], P('tensor', 'dp')
Inputs may be any that keep to these rules, and one draw needn't show every extreme that they name: `counts`: in every column some group has exactly 2 images of that size; every group has at least one image of each size.
All inputs are finite; a program needn't handle non-finite values.
Results may differ from a plain program's by a relative error of at most 0.015.
Values may be sent and summed in bfloat16 or wider, within the bound.
A program may use at most 192 MiB of HBM per device.

v0:
```python
import jax
import jax.numpy as jnp
from jax import lax
from jax.sharding import PartitionSpec as P

D = 768
HEADS = 12
HEAD_DIM = 64
FF = 3072
SIDE_S = 12
SIDE_M = 15
SIDE_L = 20
BLOCK = 512
TOK_DEV = 2048
EPSILON = 1e-06


def layout(group_counts):
    positions = jnp.arange(TOK_DEV, dtype=jnp.int32)
    area_small = SIDE_S * SIDE_S
    area_middle = SIDE_M * SIDE_M
    area_large = SIDE_L * SIDE_L
    end_small = group_counts[0] * area_small
    end_middle = end_small + group_counts[1] * area_middle
    end_large = end_middle + group_counts[2] * area_large
    size_class = (positions >= end_small).astype(jnp.int32) + (positions >= end_middle).astype(
        jnp.int32
    )
    begins = jnp.where(size_class == 0, 0, jnp.where(size_class == 1, end_small, end_middle))
    area_len = jnp.where(
        size_class == 0, area_small, jnp.where(size_class == 1, area_middle, area_large)
    )
    side_len = jnp.where(size_class == 0, SIDE_S, jnp.where(size_class == 1, SIDE_M, SIDE_L))
    within = positions - begins
    picture_index = within // area_len
    within_image = within % area_len
    is_valid = positions < end_large
    segment = jnp.where(is_valid, size_class * 16 + picture_index, 255)
    grid_row = (within_image // side_len).astype(jnp.float32)
    grid_col = (within_image % side_len).astype(jnp.float32)
    return (segment, grid_row, grid_col, is_valid.astype(jnp.float32))


def normalize(values, gain_row, shift_row):
    centred = values - jnp.mean(values, axis=-1, keepdims=True)
    spread = jnp.mean(centred * centred, axis=-1, keepdims=True)
    return centred * lax.rsqrt(spread + EPSILON) * gain_row + shift_row


def slopes_of(first_head, count_heads):
    head_number = (first_head + jnp.arange(count_heads, dtype=jnp.int32)).astype(jnp.float32) + 1.0
    return jnp.exp2(-8.0 * head_number / HEADS)


def distances(row_query, col_query, row_key, col_key):
    delta_row = row_query[:, None] - row_key[None, :]
    delta_col = col_query[:, None] - col_key[None, :]
    return jnp.sqrt(delta_row * delta_row + delta_col * delta_col)


def on_device(
    patches,
    counts,
    norm_gain,
    norm_bias,
    w_qkv,
    b_qv,
    w_out,
    out_bias,
    w_up,
    b_up,
    w_down,
    cotangent,
):
    local_rows = patches.shape[0]
    width_here = w_qkv.shape[2]
    heads_here = width_here // HEAD_DIM
    ff_here = w_up.shape[1]
    tensor_pos = lax.axis_index("tensor")
    score_scale = HEAD_DIM ** (-0.5)
    block_count = TOK_DEV // BLOCK
    segment, grid_row, grid_col, is_valid = layout(counts[0])
    keep_rows = lax.dynamic_slice_in_dim(is_valid, tensor_pos * local_rows, local_rows)[:, None]
    slopes = slopes_of(tensor_pos * heads_here, heads_here)
    inputs = patches.astype(jnp.float32)
    normed_local = normalize(inputs, norm_gain[0], norm_bias[0]).astype(jnp.bfloat16)
    normed = lax.all_gather(normed_local, "tensor", axis=0, tiled=True)
    projected = jnp.einsum("td,dsc->tsc", normed, w_qkv, preferred_element_type=jnp.float32)
    queries = (projected[:, 0] + b_qv[0]).astype(jnp.bfloat16)
    key_heads = projected[:, 1].astype(jnp.bfloat16).reshape(TOK_DEV, heads_here, HEAD_DIM)
    value_heads = (
        (projected[:, 2] + b_qv[1]).astype(jnp.bfloat16).reshape(TOK_DEV, heads_here, HEAD_DIM)
    )

    def block_scores(offset):
        query_block = lax.dynamic_slice_in_dim(queries, offset, BLOCK).reshape(
            BLOCK, heads_here, HEAD_DIM
        )
        raw_scores = (
            jnp.einsum("qhe,khe->hqk", query_block, key_heads, preferred_element_type=jnp.float32)
            * score_scale
        )
        near_dist = distances(
            lax.dynamic_slice_in_dim(grid_row, offset, BLOCK),
            lax.dynamic_slice_in_dim(grid_col, offset, BLOCK),
            grid_row,
            grid_col,
        )
        same_image = lax.dynamic_slice_in_dim(segment, offset, BLOCK)[:, None] == segment[None, :]
        return (
            query_block,
            jnp.where(
                same_image[None], raw_scores - slopes[:, None, None] * near_dist[None], -1e30
            ),
        )

    def attend_block(block_index):
        _, scores = block_scores(block_index * BLOCK)
        highest_score = jnp.max(scores, axis=-1, keepdims=True)
        exp_terms = jnp.exp(scores - highest_score)
        totals = jnp.sum(exp_terms, axis=-1, keepdims=True)
        weights = (exp_terms / totals).astype(jnp.bfloat16)
        mixed_block = jnp.einsum(
            "hqk,khe->qhe", weights, value_heads, preferred_element_type=jnp.float32
        )
        return (
            mixed_block.reshape(BLOCK, width_here).astype(jnp.bfloat16),
            highest_score[..., 0] + jnp.log(totals[..., 0]),
        )

    mixed_blocks, log_totals = lax.map(attend_block, jnp.arange(block_count, dtype=jnp.int32))
    mixed_rows = mixed_blocks.reshape(TOK_DEV, width_here)
    attended = lax.psum_scatter(
        jnp.dot(mixed_rows, w_out, preferred_element_type=jnp.float32).astype(jnp.bfloat16),
        "tensor",
        scatter_dimension=0,
        tiled=True,
    ).astype(jnp.float32)
    after_attn = inputs + keep_rows * (attended + out_bias[0])
    normed_two_local = normalize(after_attn, norm_gain[1], norm_bias[1]).astype(jnp.bfloat16)
    normed_two = lax.all_gather(normed_two_local, "tensor", axis=0, tiled=True)
    hidden_pre = jnp.dot(normed_two, w_up, preferred_element_type=jnp.float32) + b_up
    hidden = jax.nn.gelu(hidden_pre, approximate=False).astype(jnp.bfloat16)
    branch = lax.psum_scatter(
        jnp.dot(hidden, w_down, preferred_element_type=jnp.float32).astype(jnp.bfloat16),
        "tensor",
        scatter_dimension=0,
        tiled=True,
    ).astype(jnp.float32)
    result = (after_attn + keep_rows * (branch + out_bias[1])).astype(jnp.bfloat16)
    upstream = cotangent.astype(jnp.float32)
    down_bias_grad = jnp.sum(keep_rows * upstream, axis=0)
    branch_grad = lax.all_gather(
        (keep_rows * upstream).astype(jnp.bfloat16), "tensor", axis=0, tiled=True
    )
    w_down_grad = jnp.einsum("tf,td->fd", hidden, branch_grad, preferred_element_type=jnp.float32)
    hidden_grad = jnp.einsum("td,fd->tf", branch_grad, w_down, preferred_element_type=jnp.float32)
    _, gelu_back = jax.vjp(lambda pre_act: jax.nn.gelu(pre_act, approximate=False), hidden_pre)
    pre_grad = gelu_back(hidden_grad)[0].astype(jnp.bfloat16)
    up_bias_grad = jnp.sum(pre_grad, axis=0, dtype=jnp.float32)
    w_up_grad = jnp.einsum("td,tf->df", normed_two, pre_grad, preferred_element_type=jnp.float32)
    normed_two_grad = lax.psum_scatter(
        jnp.einsum("tf,df->td", pre_grad, w_up, preferred_element_type=jnp.float32).astype(
            jnp.bfloat16
        ),
        "tensor",
        scatter_dimension=0,
        tiled=True,
    ).astype(jnp.float32)
    _, norm_two_back = jax.vjp(normalize, after_attn, norm_gain[1], norm_bias[1])
    through_two, gain_two_grad, shift_two_grad = norm_two_back(normed_two_grad)
    after_grad = upstream + through_two
    attn_bias_grad = jnp.sum(keep_rows * after_grad, axis=0)
    attn_local = (keep_rows * after_grad).astype(jnp.bfloat16)
    attn_grad = lax.all_gather(attn_local, "tensor", axis=0, tiled=True)
    w_out_grad = jnp.einsum("tc,td->cd", mixed_rows, attn_grad, preferred_element_type=jnp.float32)
    mixed_grad = jnp.einsum(
        "td,cd->tc", attn_grad, w_out, preferred_element_type=jnp.float32
    ).astype(jnp.bfloat16)
    mixed_heads = mixed_grad.reshape(TOK_DEV, heads_here, HEAD_DIM)

    def back_block(running, block_index):
        key_acc, value_acc = running
        offset = block_index * BLOCK
        query_block, scores = block_scores(offset)
        weights = jnp.exp(
            scores - lax.dynamic_index_in_dim(log_totals, block_index, keepdims=False)[..., None]
        )
        grad_block = lax.dynamic_slice_in_dim(mixed_heads, offset, BLOCK)
        value_acc = value_acc + jnp.einsum(
            "hqk,qhe->khe",
            weights.astype(jnp.bfloat16),
            grad_block,
            preferred_element_type=jnp.float32,
        )
        weight_grad = jnp.einsum(
            "qhe,khe->hqk", grad_block, value_heads, preferred_element_type=jnp.float32
        )
        score_grad = (
            weights * (weight_grad - jnp.sum(weights * weight_grad, axis=-1, keepdims=True))
        ).astype(jnp.bfloat16)
        query_grad_block = (
            jnp.einsum("hqk,khe->qhe", score_grad, key_heads, preferred_element_type=jnp.float32)
            * score_scale
        )
        key_acc = (
            key_acc
            + jnp.einsum(
                "hqk,qhe->khe", score_grad, query_block, preferred_element_type=jnp.float32
            )
            * score_scale
        )
        return (
            (key_acc, value_acc),
            query_grad_block.reshape(BLOCK, width_here).astype(jnp.bfloat16),
        )

    zero_heads = jnp.zeros((TOK_DEV, heads_here, HEAD_DIM), jnp.float32)
    (key_acc, value_acc), query_blocks = lax.scan(
        back_block, (zero_heads, zero_heads), jnp.arange(block_count, dtype=jnp.int32)
    )
    query_grad = query_blocks.reshape(TOK_DEV, width_here)
    key_grad = key_acc.reshape(TOK_DEV, width_here).astype(jnp.bfloat16)
    value_grad = value_acc.reshape(TOK_DEV, width_here).astype(jnp.bfloat16)
    projected_grad = jnp.stack([query_grad, key_grad, value_grad], axis=1)
    qv_bias_grad = jnp.stack(
        [
            jnp.sum(query_grad, axis=0, dtype=jnp.float32),
            jnp.sum(value_grad, axis=0, dtype=jnp.float32),
        ]
    )
    w_qkv_grad = jnp.einsum(
        "td,tsc->dsc", normed, projected_grad, preferred_element_type=jnp.float32
    )
    normed_grad = lax.psum_scatter(
        jnp.einsum("tsc,dsc->td", projected_grad, w_qkv, preferred_element_type=jnp.float32).astype(
            jnp.bfloat16
        ),
        "tensor",
        scatter_dimension=0,
        tiled=True,
    ).astype(jnp.float32)
    qv_full = lax.dynamic_update_slice_in_dim(
        jnp.zeros((2, D), jnp.float32), qv_bias_grad, tensor_pos * width_here, 1
    )
    _, norm_one_back = jax.vjp(normalize, inputs, norm_gain[0], norm_bias[0])
    through_one, gain_one_grad, shift_one_grad = norm_one_back(normed_grad)
    input_grad = (after_grad + through_one).astype(jnp.bfloat16)
    up_full = lax.dynamic_update_slice_in_dim(
        jnp.zeros((FF,), jnp.float32), up_bias_grad, tensor_pos * ff_here, 0
    )
    gains_grad, shifts_grad, outer_grad, qv_sum, up_sum = lax.psum(
        (
            jnp.stack([gain_one_grad, gain_two_grad]),
            jnp.stack([shift_one_grad, shift_two_grad]),
            jnp.stack([attn_bias_grad, down_bias_grad]),
            qv_full,
            up_full,
        ),
        ("dp", "tensor"),
    )
    qkv_part, out_part, up_part, down_part = (
        lax.psum_scatter(w_qkv_grad, "dp", scatter_dimension=0, tiled=True),
        lax.psum_scatter(w_out_grad, "dp", scatter_dimension=1, tiled=True),
        lax.psum_scatter(w_up_grad, "dp", scatter_dimension=0, tiled=True),
        lax.psum_scatter(w_down_grad, "dp", scatter_dimension=1, tiled=True),
    )
    return (
        result,
        input_grad,
        gains_grad,
        shifts_grad,
        qkv_part,
        qv_sum,
        out_part,
        outer_grad,
        up_part,
        up_sum,
        down_part,
    )


def solution(mesh):
    placed = (
        P(("dp", "tensor"), None),
        P("dp", None),
        P(),
        P(),
        P(None, None, "tensor"),
        P(None, "tensor"),
        P("tensor", None),
        P(),
        P(None, "tensor"),
        P("tensor"),
        P("tensor", None),
        P(("dp", "tensor"), None),
    )
    return jax.shard_map(
        on_device,
        mesh=mesh,
        in_specs=placed,
        out_specs=(
            P(("dp", "tensor"), None),
            P(("dp", "tensor"), None),
            P(),
            P(),
            P("dp", None, "tensor"),
            P(),
            P("tensor", "dp"),
            P(),
            P("dp", "tensor"),
            P(),
            P("tensor", "dp"),
        ),
        check_vma=False,
    )
```

profile of v0, /device:TPU:0, one launch (start us, length us, event | category | flops | bytes accessed | tf_op | source)
XLA Modules:
  0.0 811.1 jit_solution(15307755754679857029)
XLA Ops:
  19.1 26.9 %all-gather.5.cloned.1.call-done = bf16[2048,768]{1,0:T(8,128)(2,1)} async-done(((bf16[512,768]{1,0:T(8,128)(2,1)}), bf16[2048,768]{1,0:T(8,128)(2,1)}) %all-gather.5.cloned.1.call-update) | async-done | bytes 3145744 | tf_op jit(solution)/shard_map/all_gather | solution.py:87
  46.0 3.9 fusion.73
  52.4 80.2 %while.28 = (s32[]{:T(128)}, bf16[4,512,192]{1,2,0:T(8,128)(2,1)}, f32[4,3,512]{2,1,0:T(4,128)}, s32[4]{0:T(128)}, s32[2048]{0:T(1024)S(1)}, /*index=5*/bf16[204...) while((s32[]{:T(128)}, bf16[4,512,192]{1,2,0:T(8,128)(2,1)}, ...), condition=%wide.region_5.6_spmd.clone, body=%wide.region_2.5_spmd.clone.sunk | while | flops 868317696 | bytes 61567260 | solution.py:131
  62.1 4.5 fusion.132
  66.5 4.7 fusion.133
  78.5 3.6 fusion.131
  82.1 4.5 fusion.132
  86.5 4.7 fusion.133
  102.0 4.5 fusion.132
  106.5 4.7 fusion.133
  122.0 4.5 fusion.132
  126.5 4.7 fusion.133
  135.2 3.7 convolution_convert_fusion.2
  140.7 36.2 %reduce-scatter.11.cloned.1.call-done = bf16[512,768]{1,0:T(8,128)(2,1)} async-done(((bf16[2048,768]{1,0:T(8,128)(2,1)}), bf16[512,768]{1,0:T(8,128)(2,1)}) %reduce-scatter.11.cloned.1.call-update) | async-done | bytes 786448 | tf_op jit(solution)/shard_map/reduce_scatter | solution.py:133
  184.6 28.0 %all-gather.7.cloned.1.call-done = bf16[2048,768]{1,0:T(8,128)(2,1)} async-done(((bf16[512,768]{1,0:T(8,128)(2,1)}), bf16[2048,768]{1,0:T(8,128)(2,1)}) %all-gather.7.cloned.1.call-update) | async-done | bytes 3145744 | tf_op jit(solution)/shard_map/all_gather | solution.py:141
  212.6 7.5 fusion.74
  220.1 23.0 %all-gather.9.cloned.1.call-done = bf16[2048,768]{1,0:T(8,128)(2,1)} async-done(((bf16[512,768]{1,0:T(8,128)(2,1)}), bf16[2048,768]{1,0:T(8,128)(2,1)}) %all-gather.9.cloned.1.call-update) | async-done | bytes 3145744 | tf_op jit(solution)/shard_map/all_gather | solution.py:153
  243.2 20.2 %convert_reduce_fusion = (f32[768]{0:T(1024)}, bf16[2048,768]{1,0:T(8,128)(2,1)S(1)}, f32[2048,768]{1,0:T(8,128)}) fusion(f32[2048,768]{1,0:T(8,128)} %fusion.74, f32[768]{0:T(1024)} %param.25, bf16[2048,768]{1,0:T(8,128)(2,1)} %all-gather.9.cloned.1.call-done, bf16[768,768]{1,0:T(8,128)(2,1)S(1)} %copy-done), kind=kOutput, calls=%fused_computation.43 | convolution fusion | flops 2533883136 | bytes 20060160 | tf_op jit(solution)/shard_map/td,fd->tf/dot_general | solution.py:157
  265.0 4.0 convolution_convert_fusion
  269.1 5.5 multiply_convert_fusion.1
  276.3 4.0 convolution_convert_fusion.1
  280.6 26.5 %reduce-scatter.15.cloned.1.call-done = bf16[512,768]{1,0:T(8,128)(2,1)} async-done(((bf16[2048,768]{1,0:T(8,128)(2,1)}), bf16[512,768]{1,0:T(8,128)(2,1)}) %reduce-scatter.15.cloned.1.call-update) | async-done | bytes 786448 | tf_op jit(solution)/shard_map/reduce_scatter | solution.py:162
  309.8 37.6 %reduce-scatter.13.cloned.1.call-done = bf16[512,768]{1,0:T(8,128)(2,1)} async-done(((bf16[2048,768]{1,0:T(8,128)(2,1)}), bf16[512,768]{1,0:T(8,128)(2,1)}) %reduce-scatter.13.cloned.1.call-update) | async-done | bytes 786448 | tf_op jit(solution)/shard_map/reduce_scatter | solution.py:144
  354.0 28.6 %all-gather.11.cloned.1.call-done = bf16[2048,768]{1,0:T(8,128)(2,1)} async-done(((bf16[512,768]{1,0:T(8,128)(2,1)}), bf16[2048,768]{1,0:T(8,128)(2,1)}) %all-gather.11.cloned.1.call-update) | async-done | bytes 3145744 | tf_op jit(solution)/shard_map/all_gather | solution.py:175
  382.6 4.1 convolution_bitcast_fusion
  386.8 4.0 convolution_convert_fusion.3
  391.7 141.8 %while.29 = (s32[]{:T(128)}, f32[2048,3,64]{0,2,1:T(8,128)}, f32[2048,3,64]{0,2,1:T(8,128)}, bf16[4,512,192]{1,2,0:T(8,128)(2,1)}, s32[4]{0:T(128)S(1)}, /*index...) while((s32[]{:T(128)}, f32[2048,3,64]{0,2,1:T(8,128)}, ...), condition=%wide.region_15.16_spmd.clone, body=%wide.region_13.15_spmd.clone.sunk | while | flops 2056321536 | bytes 143663600 | solution.py:219
  401.9 8.7 %multiply_reduce_fusion.4 = (f32[3,512]{1,0:T(4,128)S(1)}, f32[3,512,2048]{2,1,0:T(8,128)}) fusion(f32[3,512,2048]{2,1,0:T(8,128)S(1)} %fusion.144, f32[3,512]{1,0:T(4,128)S(1)} %dynamic-slice_bitcast_fusion.2, f32[512,2048]{1,0:T(8,128)S(1)} %add_sqrt_fusion.5, f32[3]{0:T(128)S(1)} %multiply_exponential_fusion.5, ...), kind=kOutput, calls=%fused_computation.18.clone.1 | convolution fusion | flops 424671744 | bytes 31404044 | tf_op jit(solution)/shard_map/while/body/eval_jaxpr/qhe,khe->hqk/dot_general | solution.py:100
  410.6 5.6 multiply_convert_fusion.4
  416.3 6.2 fusion.146
  437.4 8.7 %multiply_reduce_fusion.4 = (f32[3,512]{1,0:T(4,128)S(1)}, f32[3,512,2048]{2,1,0:T(8,128)}) fusion(f32[3,512,2048]{2,1,0:T(8,128)S(1)} %fusion.144, f32[3,512]{1,0:T(4,128)S(1)} %dynamic-slice_bitcast_fusion.2, f32[512,2048]{1,0:T(8,128)S(1)} %add_sqrt_fusion.5, f32[3]{0:T(128)S(1)} %multiply_exponential_fusion.5, ...), kind=kOutput, calls=%fused_computation.18.clone.1 | convolution fusion | flops 424671744 | bytes 31404044 | tf_op jit(solution)/shard_map/while/body/eval_jaxpr/qhe,khe->hqk/dot_general | solution.py:100
  446.1 5.6 multiply_convert_fusion.4
  451.7 6.1 fusion.146
  472.8 8.7 %multiply_reduce_fusion.4 = (f32[3,512]{1,0:T(4,128)S(1)}, f32[3,512,2048]{2,1,0:T(8,128)}) fusion(f32[3,512,2048]{2,1,0:T(8,128)S(1)} %fusion.144, f32[3,512]{1,0:T(4,128)S(1)} %dynamic-slice_bitcast_fusion.2, f32[512,2048]{1,0:T(8,128)S(1)} %add_sqrt_fusion.5, f32[3]{0:T(128)S(1)} %multiply_exponential_fusion.5, ...), kind=kOutput, calls=%fused_computation.18.clone.1 | convolution fusion | flops 424671744 | bytes 31404044 | tf_op jit(solution)/shard_map/while/body/eval_jaxpr/qhe,khe->hqk/dot_general | solution.py:100
  481.5 5.6 multiply_convert_fusion.4
  487.1 6.1 fusion.146
  508.2 8.7 %multiply_reduce_fusion.4 = (f32[3,512]{1,0:T(4,128)S(1)}, f32[3,512,2048]{2,1,0:T(8,128)}) fusion(f32[3,512,2048]{2,1,0:T(8,128)S(1)} %fusion.144, f32[3,512]{1,0:T(4,128)S(1)} %dynamic-slice_bitcast_fusion.2, f32[512,2048]{1,0:T(8,128)S(1)} %add_sqrt_fusion.5, f32[3]{0:T(128)S(1)} %multiply_exponential_fusion.5, ...), kind=kOutput, calls=%fused_computation.18.clone.1 | convolution fusion | flops 424671744 | bytes 31404044 | tf_op jit(solution)/shard_map/while/body/eval_jaxpr/qhe,khe->hqk/dot_general | solution.py:100
  516.9 5.6 multiply_convert_fusion.4
  522.5 6.1 fusion.146
  540.0 5.7 bitcast_convert_fusion
  545.8 7.0 fusion.76
  552.9 7.8 fusion.75
  561.0 6.0 fusion.32
  576.5 7.3 reduce-scatter.17.cloned.1.call-done
  590.2 41.6 %all-reduce = (f32[2,768]{1,0:T(2,128)}, f32[2,768]{1,0:T(2,128)}, f32[2,768]{1,0:T(2,128)}, f32[2,768]{1,0:T(2,128)}, f32[3072]{0:T(1024)}) all-reduce(f32[2,768]{1,0:T(2,128)} %pad_maximum_fusion.3, f32[2,768]{1,0:T(2,128)} %pad_maximum_fusion.4, ...), channel_id=1, replica_groups=mesh['dp'=8,'tensor'=4] {'dp','tensor'}, use_global_device_ids=true, to_apply=%region_21.22 | all-reduce | flops 9216 | bytes 73728 | tf_op jit(solution)/shard_map/psum | solution.py:252
  635.5 22.4 %reduce-scatter.23.cloned.1.call-done = f32[768,96]{0,1:T(8,128)} async-done(((f32[768,768]{0,1:T(8,128)}), f32[768,96]{0,1:T(8,128)}) %reduce-scatter.23.cloned.1.call-update) | async-done | bytes 294928 | tf_op jit(solution)/shard_map/reduce_scatter | solution.py:266
  658.0 72.9 %reduce-scatter.21.cloned.1.call-done = f32[96,768]{1,0:T(8,128)} async-done(((f32[768,768]{1,0:T(8,128)}), f32[96,768]{1,0:T(8,128)}) %reduce-scatter.21.cloned.1.call-update) | async-done | bytes 294928 | tf_op jit(solution)/shard_map/reduce_scatter | solution.py:265
  730.9 72.9 %reduce-scatter.19.cloned.1.call-done = f32[96,3,192]{2,0,1:T(8,128)} async-done(((f32[768,3,192]{2,0,1:T(8,128)}), f32[96,3,192]{2,0,1:T(8,128)}) %reduce-scatter.19.cloned.1.call-update) | async-done | bytes 221200 | tf_op jit(solution)/shard_map/reduce_scatter | solution.py:263
  (324 shorter events, 150.5 us)
Async XLA Ops:
  7.2 236.0 %copy-start = (bf16[768,768]{1,0:T(8,128)(2,1)S(1)}, bf16[768,768]{1,0:T(8,128)(2,1)}, u32[]{:S(2)}) copy-start(bf16[768,768]{1,0:T(8,128)(2,1)} %param.26) | copy-start | bytes 3538948
  7.2 7.5 copy-start.52
  7.2 8.2 %copy-start.51 = (s32[1,3]{1,0:T(1,128)S(1)}, s32[1,3]{1,0:T(1,128)}, u32[]{:S(2)}) copy-start(s32[1,3]{1,0:T(1,128)} %param.17) | copy-start | bytes 40
  7.2 38.8 %copy-start.54 = (bf16[768,3,192]{0,2,1:T(8,128)(2,1)S(1)}, bf16[768,3,192]{0,2,1:T(8,128)(2,1)}, u32[]{:S(2)}) copy-start(bf16[768,3,192]{0,2,1:T(8,128)(2,1)} %param.20) | copy-start | bytes 2654212
  7.2 38.8 %all-gather.5.cloned.1.call-start = ((), (), s32[]{:S(2)}) async-start(), calls=%async_computation.8 | async-start | bytes 3932160 | tf_op jit(solution)/shard_map/all_gather | solution.py:87
  8.7 41.2 %copy-start.31 = (f32[512]{0:T(512)}, f32[512]{0:T(512)S(1)}, u32[]{:S(2)}) copy-start(f32[512]{0:T(512)S(1)} %broadcast_multiply_fusion.1) | copy-start | bytes 6148
  10.8 39.1 %copy-start.37 = (f32[512]{0:T(512)}, f32[512]{0:T(512)S(1)}, u32[]{:S(2)}) copy-start(f32[512]{0:T(512)S(1)} %fusion.65) | copy-start | bytes 6148
  12.2 37.7 %copy-start.27 = (f32[768]{0:T(1024)}, f32[768]{0:T(1024)S(1)}, u32[]{:S(2)}) copy-start(f32[768]{0:T(1024)S(1)} %get-tuple-element.314) | copy-start | bytes 9220
  14.6 162.3 %reduce-scatter.11.cloned.1.call-start = ((), (), s32[]{:S(2)}) async-start(), calls=%async_computation.9 | async-start | bytes 3932160 | tf_op jit(solution)/shard_map/reduce_scatter | solution.py:133
  132.5 6.4 copy-start.14
  138.9 38.1 %copy-start.2 = (bf16[512,768]{1,0:T(8,128)(2,1)S(1)}, bf16[512,768]{1,0:T(8,128)(2,1)}, u32[]{:S(2)}) copy-start(bf16[512,768]{1,0:T(8,128)(2,1)} %param.16) | copy-start | bytes 2359300
  138.9 73.7 %all-gather.7.cloned.1.call-start = ((), (), s32[]{:S(2)}) async-start(), calls=%async_computation.10 | async-start | bytes 3932160 | tf_op jit(solution)/shard_map/all_gather | solution.py:141
  184.0 59.2 %all-gather.9.cloned.1.call-start = ((), (), s32[]{:S(2)}) async-start(), calls=%async_computation.12 | async-start | bytes 3932160 | tf_op jit(solution)/shard_map/all_gather | solution.py:153
  184.5 122.5 %reduce-scatter.15.cloned.1.call-start = ((), (), s32[]{:S(2)}) async-start(), calls=%async_computation.13 | async-start | bytes 3932160 | tf_op jit(solution)/shard_map/reduce_scatter | solution.py:162
  243.2 21.8 %copy-start.53 = (bf16[768,768]{1,0:T(8,128)(2,1)S(1)}, bf16[768,768]{1,0:T(8,128)(2,1)}, u32[]{:S(2)}) copy-start(bf16[768,768]{1,0:T(8,128)(2,1)} %param.24) | copy-start | bytes 3538948
  269.0 78.3 %reduce-scatter.13.cloned.1.call-start = ((), (), s32[]{:S(2)}) async-start(), calls=%async_computation.11 | async-start | bytes 3932160 | tf_op jit(solution)/shard_map/reduce_scatter | solution.py:144
  280.3 26.8 %copy-start.26 = (f32[768]{0:T(1024)S(1)}, f32[768]{0:T(1024)}, u32[]{:S(2)}) copy-start(f32[768]{0:T(1024)} %get-tuple-element.231) | copy-start | bytes 9220
  280.3 26.8 %copy-start.30 = (f32[512]{0:T(512)S(1)}, f32[512]{0:T(512)}, u32[]{:S(2)}) copy-start(f32[512]{0:T(512)} %dynamic-slice_convert_fusion) | copy-start | bytes 6148
  280.3 26.8 %copy-start.33 = (f32[768]{0:T(1024)S(1)}, f32[768]{0:T(1024)}, u32[]{:S(2)}) copy-start(f32[768]{0:T(1024)} %get-tuple-element.313) | copy-start | bytes 9220
  280.3 26.8 %copy-start.35 = (f32[512]{0:T(512)S(1)}, f32[512]{0:T(512)}, u32[]{:S(2)}) copy-start(f32[512]{0:T(512)} %copy-done.34) | copy-start | bytes 6148
  280.3 26.8 %copy-start.40 = (f32[512]{0:T(512)S(1)}, f32[512]{0:T(512)}, u32[]{:S(2)}) copy-start(f32[512]{0:T(512)} %copy-done.39) | copy-start | bytes 6148
  280.3 29.5 %copy-start.44 = (f32[512]{0:T(512)S(1)}, f32[512]{0:T(512)}, u32[]{:S(2)}) copy-start(f32[512]{0:T(512)} %copy-done.43) | copy-start | bytes 6148
  280.3 67.0 %copy-start.46 = (f32[768]{0:T(1024)S(1)}, f32[768]{0:T(1024)}, u32[]{:S(2)}) copy-start(f32[768]{0:T(1024)} %get-tuple-element.230) | copy-start | bytes 9220
  280.4 102.2 %all-gather.11.cloned.1.call-start = ((), (), s32[]{:S(2)}) async-start(), calls=%async_computation.14 | async-start | bytes 3932160 | tf_op jit(solution)/shard_map/all_gather | solution.py:175
  309.8 42.1 %copy-start.15 = (bf16[512,768]{1,0:T(8,128)(2,1)S(1)}, bf16[512,768]{1,0:T(8,128)(2,1)}, u32[]{:S(2)}) copy-start(bf16[512,768]{1,0:T(8,128)(2,1)} %param.27) | copy-start | bytes 2359300
  350.7 31.9 %copy-start.18 = (bf16[4,24,8,512]{3,2,0,1:T(8,128)(2,1)S(1)}, bf16[4,24,8,512]{3,2,0,1:T(8,128)(2,1)}, u32[]{:S(2)}) copy-start(bf16[4,24,8,512]{3,2,0,1:T(8,128)(2,1)} %copy-done.17) | copy-start | bytes 2359300
  350.7 36.0 %copy-start.41 = (f32[512]{0:T(512)}, f32[512]{0:T(512)S(1)}, u32[]{:S(2)}) copy-start(f32[512]{0:T(512)S(1)} %negate_multiply_fusion.2) | copy-start | bytes 6148
  353.9 221.0 %reduce-scatter.25.cloned.1.call-start = ((), (), s32[]{:S(2)}) async-start(), calls=%async_computation.19 | async-start | bytes 884736
  354.0 32.8 %copy-start.24 = (bf16[192,768]{1,0:T(8,128)(2,1)S(1)}, bf16[192,768]{1,0:T(8,128)(2,1)}, u32[]{:S(2)}) copy-start(bf16[192,768]{1,0:T(8,128)(2,1)} %param.22) | copy-start | bytes 884740
  386.7 197.1 %reduce-scatter.17.cloned.1.call-start = ((), (), s32[]{:S(2)}) async-start(), calls=%async_computation.15 | async-start | bytes 3932160 | tf_op jit(solution)/shard_map/reduce_scatter | solution.py:235
  410.6 5.6 copy-start.6
  446.1 5.6 copy-start.6
  481.5 5.6 copy-start.6
  516.9 5.6 copy-start.6
  545.8 112.2 %reduce-scatter.23.cloned.1.call-start = ((), (), s32[]{:S(2)}) async-start(), calls=%async_computation.18 | async-start | bytes 2654208 | tf_op jit(solution)/shard_map/reduce_scatter | solution.py:266
  552.8 8.2 %copy-start.21 = (bf16[2048,3,64]{0,2,1:T(8,128)(2,1)S(1)}, bf16[2048,3,64]{0,2,1:T(8,128)(2,1)}, u32[]{:S(2)}) copy-start(bf16[2048,3,64]{0,2,1:T(8,128)(2,1)} %convert_element_type.191) | copy-start | bytes 2359300
  552.8 8.2 %copy-start.23 = (bf16[2048,3,64]{0,2,1:T(8,128)(2,1)S(1)}, bf16[2048,3,64]{0,2,1:T(8,128)(2,1)}, u32[]{:S(2)}) copy-start(bf16[2048,3,64]{0,2,1:T(8,128)(2,1)} %copy-done.22) | copy-start | bytes 2359300
  552.8 178.1 %reduce-scatter.21.cloned.1.call-start = ((), (), s32[]{:S(2)}) async-start(), calls=%async_computation.17 | async-start | bytes 2654208 | tf_op jit(solution)/shard_map/reduce_scatter | solution.py:265
  560.7 8.7 %copy-start.45 = (f32[768]{0:T(1024)S(1)}, f32[768]{0:T(1024)}, u32[]{:S(2)}) copy-start(f32[768]{0:T(1024)} %get-tuple-element.229) | copy-start | bytes 9220
  560.7 12.1 %copy-start.16 = (bf16[4,512,192]{1,2,0:T(8,128)(2,1)S(1)}, bf16[4,512,192]{1,2,0:T(8,128)(2,1)}, u32[]{:S(2)}) copy-start(bf16[4,512,192]{1,2,0:T(8,128)(2,1)} %get-tuple-element.145) | copy-start | bytes 2359300
  560.7 243.1 %reduce-scatter.19.cloned.1.call-start = ((), (), s32[]{:S(2)}) async-start(), calls=%async_computation.16 | async-start | bytes 2654208 | tf_op jit(solution)/shard_map/reduce_scatter | solution.py:263
  567.1 16.7 %copy-start.3 = (bf16[512,768]{1,0:T(8,128)(2,1)S(1)}, bf16[512,768]{1,0:T(8,128)(2,1)}, u32[]{:S(2)}) copy-start(bf16[512,768]{1,0:T(8,128)(2,1)} %param.16) | copy-start | bytes 2359300
  567.1 16.7 %copy-start.28 = (f32[768]{0:T(1024)S(1)}, f32[768]{0:T(1024)}, u32[]{:S(2)}) copy-start(f32[768]{0:T(1024)} %copy-done.27) | copy-start | bytes 9220
  567.1 16.7 %copy-start.32 = (f32[512]{0:T(512)S(1)}, f32[512]{0:T(512)}, u32[]{:S(2)}) copy-start(f32[512]{0:T(512)} %copy-done.31) | copy-start | bytes 6148
  567.1 19.2 %copy-start.38 = (f32[512]{0:T(512)S(1)}, f32[512]{0:T(512)}, u32[]{:S(2)}) copy-start(f32[512]{0:T(512)} %copy-done.37) | copy-start | bytes 6148
  567.1 65.5 %copy-start.13 = (f32[512,768]{1,0:T(8,128)S(1)}, f32[512,768]{1,0:T(8,128)}, u32[]{:S(2)}) copy-start(f32[512,768]{1,0:T(8,128)} %copy-done.12) | copy-start | bytes 4718596
  583.8 5.8 copy-start.47
  585.5 218.3 %copy-start.1 = (bf16[768,768]{1,0:T(8,128)(2,1)S(1)}, bf16[768,768]{1,0:T(8,128)(2,1)}, u32[]{:S(2)}) copy-start(bf16[768,768]{1,0:T(8,128)(2,1)} %param.26) | copy-start | bytes 3538948
  (35 other events, 89.8 us)
Sparse Core Ops, SparseCore 0:
  14.8 31.2 all-gather.4
  139.1 37.8 reduce-scatter.10
  184.1 28.4 all-gather.6
  214.6 28.4 all-gather.8
  269.1 37.8 reduce-scatter.14
  309.5 37.8 reduce-scatter.12
  354.0 28.4 all-gather.10
  386.8 63.2 reduce-scatter.24
  545.9 37.8 reduce-scatter.16
  587.7 70.1 reduce-scatter.22
  662.0 68.8 reduce-scatter.20
  734.8 68.9 reduce-scatter.18
where the time goes:
time: 816 us; the launch traced here: 811 us
  waiting for transfers between devices  383 us (47%)
  matrix products  195 us (24%)
  other arithmetic  106 us (13%)
  local copies, waits for them, and re-layouts  52.8 us (6%)
  blocking collectives  41.6 us (5%)
  between operations  17.1 us (2%)
  loops' own time  14 us (2%)
    reduce_scatter x1, waiting for transfers between devices, on_device(): lax.psum_scatter(w_up_grad, 'dp', scatter_dimension=0, tiled=True)  72.9 us
    reduce_scatter x1, waiting for transfers between devices, on_device(): lax.psum_scatter(w_qkv_grad, 'dp', scatter_dimension=0, tiled=True)  72.9 us
    dot_general x8, matrix products, block_scores(): jnp.einsum('qhe,khe->hqk', query_block, key_heads, preferred_element_type...  49.1 us
    psum x1, blocking collectives, on_device(): lax.psum((jnp.stack([gain_one_grad, gain_two_grad]), jnp.stack([shift_one...  41.6 us
    reduce_scatter x1, waiting for transfers between devices, on_device(): lax.psum_scatter(jnp.dot(hidden, w_down, preferred_element_type=jnp.float...  37.6 us
    reduce_scatter x1, waiting for transfers between devices, on_device(): lax.psum_scatter(jnp.dot(mixed_rows, w_out, preferred_element_type=jnp.fl...  36.2 us
    all_gather x1, waiting for transfers between devices, on_device(): attn_grad = lax.all_gather(attn_local, 'tensor', axis=0, tiled=True)  28.6 us
    all_gather x1, waiting for transfers between devices, on_device(): normed_two = lax.all_gather(normed_two_local, 'tensor', axis=0, tiled=True)  28 us
  transfers between devices with their start and end apart: 12, of which 11 were waited for; matrix products, arithmetic and copies ran while one was open for 26% of the time, Pallas kernels for 0%

commit v1 on v0

--- a/solution.py
+++ b/solution.py
@@ -13,6 +13,12 @@
 BLOCK = 512
 TOK_DEV = 2048
 EPSILON = 1e-06
+
+
+def laid_out(blocks, dim):
+    lengths = list(blocks.shape[1:])
+    lengths[dim] *= blocks.shape[0]
+    return jnp.moveaxis(blocks, 0, dim).reshape(lengths)
 
 
 def layout(group_counts):
@@ -172,7 +178,19 @@
     after_grad = upstream + through_two
     attn_bias_grad = jnp.sum(keep_rows * after_grad, axis=0)
     attn_local = (keep_rows * after_grad).astype(jnp.bfloat16)
-    attn_grad = lax.all_gather(attn_local, "tensor", axis=0, tiled=True)
+    size = lax.axis_size("tensor")
+    pairs = [(i, (i + 1) % size) for i in range(size)]
+    back = [(b, a) for a, b in pairs]
+    lower, upper = ([], [])
+    for step in range(size - 1):
+        if step % 2 == 0:
+            lower.append(lax.ppermute(lower[-1] if lower else attn_local, "tensor", pairs))
+        else:
+            upper.append(lax.ppermute(upper[-1] if upper else attn_local, "tensor", back))
+    tiles = jnp.stack([*lower[::-1], attn_local, *upper])
+    shift = lax.axis_index("tensor") - len(lower)
+    tiles = tiles[(jnp.arange(size) - shift) % size]
+    attn_grad = laid_out(tiles, 0)
     w_out_grad = jnp.einsum("tc,td->cd", mixed_rows, attn_grad, preferred_element_type=jnp.float32)
     mixed_grad = jnp.einsum(
         "td,cd->tc", attn_grad, w_out, preferred_element_type=jnp.float32

time: 816 us -> 822 us (level)
    ppermute x0 -> x3, waiting for transfers between devices: none -> 28.9 us  [the longest x2 28.9 us: on_device(): lax.ppermute(lower[-1] if lower else attn_local, 'tensor', pairs)]
    all_gather x1 -> x0, waiting for transfers between devices: 28.6 us -> none  [on_device(): attn_grad = lax.all_gather(attn_local, 'tensor', axis=0, tiled=True)]
  transfers between devices with their start and end apart: 12 -> 14, of which waited for: 11 -> 12; matrix products, arithmetic and copies ran while one was open for 26% -> 26% of each run, Pallas kernels for 0% -> 0%
where the time goes in v1:
time: 822 us; the launch traced here: 817 us
  waiting for transfers between devices  382 us (46%)
  matrix products  195 us (24%)
  other arithmetic  108 us (13%)
  local copies, waits for them, and re-layouts  56.2 us (7%)
  blocking collectives  41.8 us (5%)
  between operations  16.8 us (2%)
  loops' own time  14 us (2%)
    reduce_scatter x1, waiting for transfers between devices, on_device(): lax.psum_scatter(w_qkv_grad, 'dp', scatter_dimension=0, tiled=True)  72.9 us
    reduce_scatter x1, waiting for transfers between devices, on_device(): lax.psum_scatter(w_up_grad, 'dp', scatter_dimension=0, tiled=True)  72.7 us
    dot_general x8, matrix products, block_scores(): jnp.einsum('qhe,khe->hqk', query_block, key_heads, preferred_element_type...  49.1 us
    psum x1, blocking collectives, on_device(): lax.psum((jnp.stack([gain_one_grad, gain_two_grad]), jnp.stack([shift_one...  41.8 us
    reduce_scatter x1, waiting for transfers between devices, on_device(): lax.psum_scatter(jnp.dot(hidden, w_down, preferred_element_type=jnp.float...  37.6 us
    reduce_scatter x1, waiting for transfers between devices, on_device(): lax.psum_scatter(jnp.dot(mixed_rows, w_out, preferred_element_type=jnp.fl...  36.2 us
    ppermute x2, waiting for transfers between devices, on_device(): lax.ppermute(lower[-1] if lower else attn_local, 'tensor', pairs)  28.9 us
    all_gather x1, waiting for transfers between devices, on_device(): normed_two = lax.all_gather(normed_two_local, 'tensor', axis=0, tiled=True)  28 us
  transfers between devices with their start and end apart: 14, of which 12 were waited for; matrix products, arithmetic and copies ran while one was open for 26% of the time, Pallas kernels for 0%

profile of v1, /device:TPU:0, one launch (start us, length us, event | category | flops | bytes accessed | tf_op | source)
XLA Modules:
  0.0 817.1 jit_solution(8024319856887951667)
XLA Ops:
  19.1 26.9 %all-gather.4.cloned.1.call-done = bf16[2048,768]{1,0:T(8,128)(2,1)} async-done(((bf16[512,768]{1,0:T(8,128)(2,1)}), bf16[2048,768]{1,0:T(8,128)(2,1)}) %all-gather.4.cloned.1.call-update) | async-done | bytes 3145744 | tf_op jit(solution)/shard_map/all_gather | solution.py:93
  46.0 3.9 fusion.75
  52.4 80.2 %while.28 = (s32[]{:T(128)}, bf16[4,512,192]{1,2,0:T(8,128)(2,1)}, f32[4,3,512]{2,1,0:T(4,128)}, s32[4]{0:T(128)}, s32[2048]{0:T(1024)S(1)}, /*index=5*/bf16[204...) while((s32[]{:T(128)}, bf16[4,512,192]{1,2,0:T(8,128)(2,1)}, ...), condition=%wide.region_5.6_spmd.clone, body=%wide.region_2.5_spmd.clone.sunk | while | flops 868317696 | bytes 61567260 | solution.py:137
  62.1 4.5 fusion.134
  66.5 4.7 fusion.135
  82.1 4.5 fusion.134
  86.5 4.7 fusion.135
  102.1 4.5 fusion.134
  106.5 4.7 fusion.135
  122.0 4.5 fusion.134
  126.5 4.7 fusion.135
  139.9 36.2 %reduce-scatter.11.cloned.1.call-done = bf16[512,768]{1,0:T(8,128)(2,1)} async-done(((bf16[2048,768]{1,0:T(8,128)(2,1)}), bf16[512,768]{1,0:T(8,128)(2,1)}) %reduce-scatter.11.cloned.1.call-update) | async-done | bytes 786448 | tf_op jit(solution)/shard_map/reduce_scatter | solution.py:139
  183.7 28.0 %all-gather.6.cloned.1.call-done = bf16[2048,768]{1,0:T(8,128)(2,1)} async-done(((bf16[512,768]{1,0:T(8,128)(2,1)}), bf16[2048,768]{1,0:T(8,128)(2,1)}) %all-gather.6.cloned.1.call-update) | async-done | bytes 3145744 | tf_op jit(solution)/shard_map/all_gather | solution.py:147
  211.7 7.5 fusion.76
  219.2 22.5 %all-gather.8.cloned.1.call-done = bf16[2048,768]{1,0:T(8,128)(2,1)} async-done(((bf16[512,768]{1,0:T(8,128)(2,1)}), bf16[2048,768]{1,0:T(8,128)(2,1)}) %all-gather.8.cloned.1.call-update) | async-done | bytes 3145744 | tf_op jit(solution)/shard_map/all_gather | solution.py:159
  241.7 20.2 %convert_reduce_fusion = (f32[768]{0:T(1024)}, bf16[2048,768]{1,0:T(8,128)(2,1)S(1)}, f32[2048,768]{1,0:T(8,128)}) fusion(f32[2048,768]{1,0:T(8,128)} %fusion.76, f32[768]{0:T(1024)} %param.25, bf16[2048,768]{1,0:T(8,128)(2,1)} %all-gather.8.cloned.1.call-done, bf16[768,768]{1,0:T(8,128)(2,1)S(1)} %copy-done), kind=kOutput, calls=%fused_computation.44 | convolution fusion | flops 2533883136 | bytes 20060160 | tf_op jit(solution)/shard_map/td,fd->tf/dot_general | solution.py:163
  263.5 4.0 convolution_convert_fusion
  267.6 5.5 multiply_convert_fusion.1
  274.8 4.0 convolution_convert_fusion.1
  279.1 26.5 %reduce-scatter.15.cloned.1.call-done = bf16[512,768]{1,0:T(8,128)(2,1)} async-done(((bf16[2048,768]{1,0:T(8,128)(2,1)}), bf16[512,768]{1,0:T(8,128)(2,1)}) %reduce-scatter.15.cloned.1.call-update) | async-done | bytes 786448 | tf_op jit(solution)/shard_map/reduce_scatter | solution.py:168
  308.3 37.6 %reduce-scatter.13.cloned.1.call-done = bf16[512,768]{1,0:T(8,128)(2,1)} async-done(((bf16[2048,768]{1,0:T(8,128)(2,1)}), bf16[512,768]{1,0:T(8,128)(2,1)}) %reduce-scatter.13.cloned.1.call-update) | async-done | bytes 786448 | tf_op jit(solution)/shard_map/reduce_scatter | solution.py:150
  353.2 17.5 %collective-permute-done = bf16[512,768]{1,0:T(8,128)(2,1)S(1)} collective-permute-done((bf16[512,768]{1,0:T(8,128)(2,1)S(1)}, bf16[512,768]{1,0:T(8,128)(2,1)S(1)}, u32[]{:S(2)}, u32[]{:S(2)}) %collective-permute-start) | collective-permute-done | bytes 786464 | tf_op jit(solution)/shard_map/ppermute | solution.py:187
  370.7 11.5 %collective-permute-done.1 = bf16[512,768]{1,0:T(8,128)(2,1)} collective-permute-done((bf16[512,768]{1,0:T(8,128)(2,1)S(1)}, bf16[512,768]{1,0:T(8,128)(2,1)}, u32[]{:S(2)}, u32[]{:S(2)}) %collective-permute-start.1) | collective-permute-done | bytes 786464 | tf_op jit(solution)/shard_map/ppermute | solution.py:187
  385.1 4.4 gather_fusion
  389.5 4.2 convolution_bitcast_fusion
  393.7 4.0 convolution_convert_fusion.3
  398.7 141.7 %while.29 = (s32[]{:T(128)}, f32[2048,3,64]{0,2,1:T(8,128)}, f32[2048,3,64]{0,2,1:T(8,128)}, bf16[4,512,192]{1,2,0:T(8,128)(2,1)}, s32[4]{0:T(128)S(1)}, /*index...) while((s32[]{:T(128)}, f32[2048,3,64]{0,2,1:T(8,128)}, ...), condition=%wide.region_15.16_spmd.clone, body=%wide.region_13.15_spmd.clone.sunk | while | flops 2056321536 | bytes 143663600 | solution.py:237
  408.9 8.7 %multiply_reduce_fusion.4 = (f32[3,512]{1,0:T(4,128)S(1)}, f32[3,512,2048]{2,1,0:T(8,128)}) fusion(f32[3,512,2048]{2,1,0:T(8,128)S(1)} %fusion.146, f32[3,512]{1,0:T(4,128)S(1)} %dynamic-slice_bitcast_fusion.2, f32[512,2048]{1,0:T(8,128)S(1)} %add_sqrt_fusion.5, f32[3]{0:T(128)S(1)} %multiply_exponential_fusion.5, ...), kind=kOutput, calls=%fused_computation.19.clone.1 | convolution fusion | flops 424671744 | bytes 31404044 | tf_op jit(solution)/shard_map/while/body/eval_jaxpr/qhe,khe->hqk/dot_general | solution.py:106
  417.6 5.6 multiply_convert_fusion.4
  423.2 6.2 fusion.148
  444.3 8.7 %multiply_reduce_fusion.4 = (f32[3,512]{1,0:T(4,128)S(1)}, f32[3,512,2048]{2,1,0:T(8,128)}) fusion(f32[3,512,2048]{2,1,0:T(8,128)S(1)} %fusion.146, f32[3,512]{1,0:T(4,128)S(1)} %dynamic-slice_bitcast_fusion.2, f32[512,2048]{1,0:T(8,128)S(1)} %add_sqrt_fusion.5, f32[3]{0:T(128)S(1)} %multiply_exponential_fusion.5, ...), kind=kOutput, calls=%fused_computation.19.clone.1 | convolution fusion | flops 424671744 | bytes 31404044 | tf_op jit(solution)/shard_map/while/body/eval_jaxpr/qhe,khe->hqk/dot_general | solution.py:106
  453.0 5.6 multiply_convert_fusion.4
  458.6 6.1 fusion.148
  479.7 8.7 %multiply_reduce_fusion.4 = (f32[3,512]{1,0:T(4,128)S(1)}, f32[3,512,2048]{2,1,0:T(8,128)}) fusion(f32[3,512,2048]{2,1,0:T(8,128)S(1)} %fusion.146, f32[3,512]{1,0:T(4,128)S(1)} %dynamic-slice_bitcast_fusion.2, f32[512,2048]{1,0:T(8,128)S(1)} %add_sqrt_fusion.5, f32[3]{0:T(128)S(1)} %multiply_exponential_fusion.5, ...), kind=kOutput, calls=%fused_computation.19.clone.1 | convolution fusion | flops 424671744 | bytes 31404044 | tf_op jit(solution)/shard_map/while/body/eval_jaxpr/qhe,khe->hqk/dot_general | solution.py:106
  488.4 5.6 multiply_convert_fusion.4
  494.0 6.1 fusion.148
  515.0 8.7 %multiply_reduce_fusion.4 = (f32[3,512]{1,0:T(4,128)S(1)}, f32[3,512,2048]{2,1,0:T(8,128)}) fusion(f32[3,512,2048]{2,1,0:T(8,128)S(1)} %fusion.146, f32[3,512]{1,0:T(4,128)S(1)} %dynamic-slice_bitcast_fusion.2, f32[512,2048]{1,0:T(8,128)S(1)} %add_sqrt_fusion.5, f32[3]{0:T(128)S(1)} %multiply_exponential_fusion.5, ...), kind=kOutput, calls=%fused_computation.19.clone.1 | convolution fusion | flops 424671744 | bytes 31404044 | tf_op jit(solution)/shard_map/while/body/eval_jaxpr/qhe,khe->hqk/dot_general | solution.py:106
  523.7 5.6 multiply_convert_fusion.4
  529.3 6.1 fusion.148
  546.9 5.7 bitcast_convert_fusion
  552.7 7.0 fusion.78
  559.8 7.7 fusion.77
  567.9 5.9 fusion.32
  583.3 7.2 reduce-scatter.17.cloned.1.call-done
  596.9 41.8 %all-reduce = (f32[2,768]{1,0:T(2,128)}, f32[2,768]{1,0:T(2,128)}, f32[2,768]{1,0:T(2,128)}, f32[2,768]{1,0:T(2,128)}, f32[3072]{0:T(1024)}) all-reduce(f32[2,768]{1,0:T(2,128)} %pad_maximum_fusion.4, f32[2,768]{1,0:T(2,128)} %pad_maximum_fusion.5, ...), channel_id=1, replica_groups=mesh['dp'=8,'tensor'=4] {'dp','tensor'}, use_global_device_ids=true, to_apply=%region_21.22 | all-reduce | flops 9216 | bytes 73728 | tf_op jit(solution)/shard_map/psum | solution.py:270
  642.4 22.2 %reduce-scatter.23.cloned.1.call-done = f32[768,96]{0,1:T(8,128)} async-done(((f32[768,768]{0,1:T(8,128)}), f32[768,96]{0,1:T(8,128)}) %reduce-scatter.23.cloned.1.call-update) | async-done | bytes 294928 | tf_op jit(solution)/shard_map/reduce_scatter | solution.py:284
  664.5 72.7 %reduce-scatter.21.cloned.1.call-done = f32[96,768]{1,0:T(8,128)} async-done(((f32[768,768]{1,0:T(8,128)}), f32[96,768]{1,0:T(8,128)}) %reduce-scatter.21.cloned.1.call-update) | async-done | bytes 294928 | tf_op jit(solution)/shard_map/reduce_scatter | solution.py:283
  737.3 72.9 %reduce-scatter.19.cloned.1.call-done = f32[96,3,192]{2,0,1:T(8,128)} async-done(((f32[768,3,192]{2,0,1:T(8,128)}), f32[96,3,192]{2,0,1:T(8,128)}) %reduce-scatter.19.cloned.1.call-update) | async-done | bytes 221200 | tf_op jit(solution)/shard_map/reduce_scatter | solution.py:281
  (329 shorter events, 160.5 us)
Async XLA Ops:
  7.2 234.5 %copy-start = (bf16[768,768]{1,0:T(8,128)(2,1)S(1)}, bf16[768,768]{1,0:T(8,128)(2,1)}, u32[]{:S(2)}) copy-start(bf16[768,768]{1,0:T(8,128)(2,1)} %param.26) | copy-start | bytes 3538948
  7.2 7.5 copy-start.51
  7.2 8.2 %copy-start.50 = (s32[1,3]{1,0:T(1,128)S(1)}, s32[1,3]{1,0:T(1,128)}, u32[]{:S(2)}) copy-start(s32[1,3]{1,0:T(1,128)} %param.17) | copy-start | bytes 40
  7.2 38.8 %copy-start.53 = (bf16[768,3,192]{0,2,1:T(8,128)(2,1)S(1)}, bf16[768,3,192]{0,2,1:T(8,128)(2,1)}, u32[]{:S(2)}) copy-start(bf16[768,3,192]{0,2,1:T(8,128)(2,1)} %param.20) | copy-start | bytes 2654212
  7.2 38.8 %all-gather.4.cloned.1.call-start = ((), (), s32[]{:S(2)}) async-start(), calls=%async_computation.8 | async-start | bytes 3932160 | tf_op jit(solution)/shard_map/all_gather | solution.py:93
  8.7 41.2 %copy-start.30 = (f32[512]{0:T(512)}, f32[512]{0:T(512)S(1)}, u32[]{:S(2)}) copy-start(f32[512]{0:T(512)S(1)} %broadcast_multiply_fusion.1) | copy-start | bytes 6148
  10.8 39.1 %copy-start.36 = (f32[512]{0:T(512)}, f32[512]{0:T(512)S(1)}, u32[]{:S(2)}) copy-start(f32[512]{0:T(512)S(1)} %fusion.65) | copy-start | bytes 6148
  12.2 37.7 %copy-start.26 = (f32[768]{0:T(1024)}, f32[768]{0:T(1024)S(1)}, u32[]{:S(2)}) copy-start(f32[768]{0:T(1024)S(1)} %get-tuple-element.314) | copy-start | bytes 9220
  14.6 161.5 %reduce-scatter.11.cloned.1.call-start = ((), (), s32[]{:S(2)}) async-start(), calls=%async_computation.9 | async-start | bytes 3932160 | tf_op jit(solution)/shard_map/reduce_scatter | solution.py:139
  132.6 5.5 copy-start.14
  138.0 38.1 %copy-start.2 = (bf16[512,768]{1,0:T(8,128)(2,1)S(1)}, bf16[512,768]{1,0:T(8,128)(2,1)}, u32[]{:S(2)}) copy-start(bf16[512,768]{1,0:T(8,128)(2,1)} %param.16) | copy-start | bytes 2359300
  138.1 73.7 %all-gather.6.cloned.1.call-start = ((), (), s32[]{:S(2)}) async-start(), calls=%async_computation.10 | async-start | bytes 3932160 | tf_op jit(solution)/shard_map/all_gather | solution.py:147
  183.1 58.6 %all-gather.8.cloned.1.call-start = ((), (), s32[]{:S(2)}) async-start(), calls=%async_computation.12 | async-start | bytes 3932160 | tf_op jit(solution)/shard_map/all_gather | solution.py:159
  183.6 121.9 %reduce-scatter.15.cloned.1.call-start = ((), (), s32[]{:S(2)}) async-start(), calls=%async_computation.13 | async-start | bytes 3932160 | tf_op jit(solution)/shard_map/reduce_scatter | solution.py:168
  241.7 21.8 %copy-start.52 = (bf16[768,768]{1,0:T(8,128)(2,1)S(1)}, bf16[768,768]{1,0:T(8,128)(2,1)}, u32[]{:S(2)}) copy-start(bf16[768,768]{1,0:T(8,128)(2,1)} %param.24) | copy-start | bytes 3538948
  267.5 78.3 %reduce-scatter.13.cloned.1.call-start = ((), (), s32[]{:S(2)}) async-start(), calls=%async_computation.11 | async-start | bytes 3932160 | tf_op jit(solution)/shard_map/reduce_scatter | solution.py:150
  278.8 26.8 %copy-start.25 = (f32[768]{0:T(1024)S(1)}, f32[768]{0:T(1024)}, u32[]{:S(2)}) copy-start(f32[768]{0:T(1024)} %get-tuple-element.231) | copy-start | bytes 9220
  278.8 26.8 %copy-start.29 = (f32[512]{0:T(512)S(1)}, f32[512]{0:T(512)}, u32[]{:S(2)}) copy-start(f32[512]{0:T(512)} %dynamic-slice_convert_fusion) | copy-start | bytes 6148
  278.8 26.8 %copy-start.32 = (f32[768]{0:T(1024)S(1)}, f32[768]{0:T(1024)}, u32[]{:S(2)}) copy-start(f32[768]{0:T(1024)} %get-tuple-element.313) | copy-start | bytes 9220
  278.8 26.8 %copy-start.34 = (f32[512]{0:T(512)S(1)}, f32[512]{0:T(512)}, u32[]{:S(2)}) copy-start(f32[512]{0:T(512)} %copy-done.33) | copy-start | bytes 6148
  278.8 26.8 %copy-start.39 = (f32[512]{0:T(512)S(1)}, f32[512]{0:T(512)}, u32[]{:S(2)}) copy-start(f32[512]{0:T(512)} %copy-done.38) | copy-start | bytes 6148
  278.8 29.5 %copy-start.43 = (f32[512]{0:T(512)S(1)}, f32[512]{0:T(512)}, u32[]{:S(2)}) copy-start(f32[512]{0:T(512)} %copy-done.42) | copy-start | bytes 6148
  278.8 67.0 %copy-start.45 = (f32[768]{0:T(1024)S(1)}, f32[768]{0:T(1024)}, u32[]{:S(2)}) copy-start(f32[768]{0:T(1024)} %get-tuple-element.230) | copy-start | bytes 9220
  278.9 302.8 %reduce-scatter.25.cloned.1.call-start = ((), (), s32[]{:S(2)}) async-start(), calls=%async_computation.18 | async-start | bytes 884736
  308.3 42.1 %copy-start.15 = (bf16[512,768]{1,0:T(8,128)(2,1)S(1)}, bf16[512,768]{1,0:T(8,128)(2,1)}, u32[]{:S(2)}) copy-start(bf16[512,768]{1,0:T(8,128)(2,1)} %param.27) | copy-start | bytes 2359300
  349.2 35.9 %copy-start.40 = (f32[512]{0:T(512)}, f32[512]{0:T(512)S(1)}, u32[]{:S(2)}) copy-start(f32[512]{0:T(512)S(1)} %negate_multiply_fusion.2) | copy-start | bytes 6148
  351.5 19.2 %collective-permute-start = (bf16[512,768]{1,0:T(8,128)(2,1)S(1)}, bf16[512,768]{1,0:T(8,128)(2,1)S(1)}, u32[]{:S(2)}, u32[]{:S(2)}) collective-permute-start(bf16[512,768]{1,0:T(8,128)(2,1)S(1)} %get-tuple-element.302), channel_id=1, source_target_pairs={{0,1},{1,2},{2,3},{3,0},{4,5},{5,6},{6,7},{7,4},{8,9},{9,10},{10,1... | collective-permute-start | bytes 2359304 | tf_op jit(solution)/shard_map/ppermute | solution.py:187
  351.5 19.2 %collective-permute-start.2 = (bf16[512,768]{1,0:T(8,128)(2,1)S(1)}, bf16[512,768]{1,0:T(8,128)(2,1)S(1)}, u32[]{:S(2)}, u32[]{:S(2)}) collective-permute-start(bf16[512,768]{1,0:T(8,128)(2,1)S(1)} %get-tuple-element.302), channel_id=1, source_target_pairs={{1,0},{2,1},{3,2},{0,3},{5,4},{6,5},{7,6},{4,7},{9,8},{10,9},{11,1... | collective-permute-start | bytes 2359304 | tf_op jit(solution)/shard_map/ppermute | solution.py:189
  370.7 11.5 %collective-permute-start.1 = (bf16[512,768]{1,0:T(8,128)(2,1)S(1)}, bf16[512,768]{1,0:T(8,128)(2,1)}, u32[]{:S(2)}, u32[]{:S(2)}) collective-permute-start(bf16[512,768]{1,0:T(8,128)(2,1)S(1)} %collective-permute-done), channel_id=1, source_target_pairs={{0,1},{1,2},{2,3},{3,0},{4,5},{5,6},{6,7},{7,4},{8,9},{9,10},{10,1... | collective-permute-start | bytes 2359304 | tf_op jit(solution)/shard_map/ppermute | solution.py:187
  393.7 196.8 %reduce-scatter.17.cloned.1.call-start = ((), (), s32[]{:S(2)}) async-start(), calls=%async_computation.14 | async-start | bytes 3932160 | tf_op jit(solution)/shard_map/reduce_scatter | solution.py:253
  417.6 5.6 copy-start.6
  453.0 5.6 copy-start.6
  488.4 5.6 copy-start.6
  523.7 5.6 copy-start.6
  552.7 111.9 %reduce-scatter.23.cloned.1.call-start = ((), (), s32[]{:S(2)}) async-start(), calls=%async_computation.17 | async-start | bytes 2654208 | tf_op jit(solution)/shard_map/reduce_scatter | solution.py:284
  559.7 8.1 copy-start.20
  559.7 8.1 copy-start.22
  559.7 177.5 %reduce-scatter.21.cloned.1.call-start = ((), (), s32[]{:S(2)}) async-start(), calls=%async_computation.16 | async-start | bytes 2654208 | tf_op jit(solution)/shard_map/reduce_scatter | solution.py:283
  567.5 8.7 %copy-start.44 = (f32[768]{0:T(1024)S(1)}, f32[768]{0:T(1024)}, u32[]{:S(2)}) copy-start(f32[768]{0:T(1024)} %get-tuple-element.229) | copy-start | bytes 9220
  567.5 12.0 %copy-start.16 = (bf16[4,512,192]{1,2,0:T(8,128)(2,1)S(1)}, bf16[4,512,192]{1,2,0:T(8,128)(2,1)}, u32[]{:S(2)}) copy-start(bf16[4,512,192]{1,2,0:T(8,128)(2,1)} %get-tuple-element.145) | copy-start | bytes 2359300
  567.6 242.6 %reduce-scatter.19.cloned.1.call-start = ((), (), s32[]{:S(2)}) async-start(), calls=%async_computation.15 | async-start | bytes 2654208 | tf_op jit(solution)/shard_map/reduce_scatter | solution.py:281
  573.8 16.7 %copy-start.3 = (bf16[512,768]{1,0:T(8,128)(2,1)S(1)}, bf16[512,768]{1,0:T(8,128)(2,1)}, u32[]{:S(2)}) copy-start(bf16[512,768]{1,0:T(8,128)(2,1)} %param.16) | copy-start | bytes 2359300
  573.8 16.7 %copy-start.27 = (f32[768]{0:T(1024)S(1)}, f32[768]{0:T(1024)}, u32[]{:S(2)}) copy-start(f32[768]{0:T(1024)} %copy-done.26) | copy-start | bytes 9220
  573.8 16.7 %copy-start.31 = (f32[512]{0:T(512)S(1)}, f32[512]{0:T(512)}, u32[]{:S(2)}) copy-start(f32[512]{0:T(512)} %copy-done.30) | copy-start | bytes 6148
  573.8 19.2 %copy-start.37 = (f32[512]{0:T(512)S(1)}, f32[512]{0:T(512)}, u32[]{:S(2)}) copy-start(f32[512]{0:T(512)} %copy-done.36) | copy-start | bytes 6148
  573.8 65.6 %copy-start.13 = (f32[512,768]{1,0:T(8,128)S(1)}, f32[512,768]{1,0:T(8,128)}, u32[]{:S(2)}) copy-start(f32[512,768]{1,0:T(8,128)} %copy-done.12) | copy-start | bytes 4718596
  590.5 5.8 copy-start.46
  592.2 217.9 %copy-start.1 = (bf16[768,768]{1,0:T(8,128)(2,1)S(1)}, bf16[768,768]{1,0:T(8,128)(2,1)}, u32[]{:S(2)}) copy-start(bf16[768,768]{1,0:T(8,128)(2,1)} %param.26) | copy-start | bytes 3538948
  (36 other events, 97.3 us)
Sparse Core Ops, SparseCore 0:
  14.8 31.2 all-gather.3
  138.2 37.8 reduce-scatter.10
  183.2 28.4 all-gather.5
  213.1 28.4 all-gather.7
  267.7 37.8 reduce-scatter.14
  308.0 37.8 reduce-scatter.12
  393.8 63.0 reduce-scatter.24
  552.8 37.6 reduce-scatter.16
  594.6 69.9 reduce-scatter.22
  668.5 68.7 reduce-scatter.20
  741.3 68.7 reduce-scatter.18
